TPU v7x, 512 devices: a whole 4x4x16 slice. The times are simulated.
512 devices in a mesh: seq: 16 (over y, z_lo), outer: 32 (over z_hi, x, core).
Axes of the slice: x: 4, y: 4, z: 16 (z_hi: 4, z_lo: 4; z = z_hi * 4 + z_lo), core: 2. Of those that a mesh axis runs over, the one named last changes fastest.
Arguments:
- queries: bfloat16 [262144, 2048], P(('outer', 'seq')), may hold values from -41 to 41
- keys: bfloat16 [262144, 512], P(('outer', 'seq')), may hold values from -6 to 6
- values: bfloat16 [262144, 512], P(('outer', 'seq')), may hold values from -6 to 6
Outputs:
- attended: bfloat16 [262144, 2048], P(('outer', 'seq'))
All inputs are finite; a program needn't handle non-finite values.
Results may differ from a plain program's by a relative error of at most 0.014.
Values may be sent and summed in bfloat16 or wider, within the bound.
No kernel may reach another device: no remote copies, remote signals or barrier semaphores. Data moves between devices by JAX's collectives and lax.ppermute only.
A program may use at most 64 MiB of HBM per device.

v0:
```python
import jax
import jax.numpy as jnp
from jax import lax
from jax.sharding import PartitionSpec as P

HD = 128
QHEADS = 16
KVHEADS = 4
BLOCK = 128
POOL = 8


def shortened(value):

    def short(part):
        return part.astype(jnp.bfloat16) if part.dtype == jnp.float32 else part

    return jax.tree.map(short, value)


def shifted(block, axis, distance):
    devices = range(lax.axis_size(axis))
    route = [((i - distance) % len(devices), i) for i in devices]
    return lax.ppermute(block, axis, route)


def shifted_2(value, axis, steps):
    count = lax.axis_size(axis)
    first, last = (max(0, -steps), min(count, count - steps))
    return lax.ppermute(value, axis, [(source, source + steps) for source in range(first, last)])


def joined_along(pieces, dim):
    pieces = jnp.moveaxis(pieces, 0, dim)
    dims = pieces.shape
    return pieces.reshape(*dims[:dim], dims[dim] * dims[dim + 1], *dims[dim + 2 :])


def copy_for_each(value, axis):
    devices = lax.axis_size(axis)
    return lax.all_to_all(
        jnp.broadcast_to(value[None], (devices, *value.shape)), axis, 0, 0, tiled=True
    )


def collect(value, axis, dim):
    return joined_along(copy_for_each(value, axis), dim)


def sent_together(arrays, axis, dim, along):
    widths = [a.shape[along] for a in arrays]
    both = jnp.concatenate(arrays, axis=along)
    result = collect(both, axis, dim)
    return tuple(jnp.split(result, [sum(widths[:k]) for k in range(1, len(widths))], axis=along))


def sent_together_2(arrays, axis, dim, along):
    widths = [a.shape[along] for a in arrays]
    both = jnp.concatenate(arrays, axis=along)
    result = lax.all_gather(both, axis, axis=dim, tiled=True)
    return tuple(jnp.split(result, [sum(widths[:k]) for k in range(1, len(widths))], axis=along))


def pool_level(element_item):
    span_length = element_item.shape[0]
    summed = (
        element_item.astype(jnp.float32)
        .reshape(span_length // POOL, POOL, element_item.shape[1])
        .sum(axis=1)
    )
    return (summed * POOL ** (-0.5)).astype(jnp.bfloat16)


def attend_block(query_rows, key_set, value_set, valid):
    group_size = QHEADS // KVHEADS
    head_queries = query_rows.reshape(BLOCK, KVHEADS, group_size, HD).transpose(1, 0, 2, 3)
    head_keys = key_set.reshape(-1, KVHEADS, HD).transpose(1, 0, 2)
    head_values = value_set.reshape(-1, KVHEADS, HD).transpose(1, 0, 2)

    def one_head(operands):
        part_q, part_k, part_v = operands
        scores = jnp.einsum(
            "tgd,sd->gts", part_q, part_k, preferred_element_type=jnp.float32
        ) * HD ** (-0.5)
        scores = jnp.where(valid, scores, -jnp.inf)
        highest = jnp.max(scores, axis=2, keepdims=True)
        weights = jnp.exp(scores - highest)
        totals = jnp.sum(weights, axis=2)
        rounded = weights.astype(jnp.bfloat16)
        mixed = jnp.einsum("gts,sd->tgd", rounded, part_v, preferred_element_type=jnp.float32)
        return (mixed / totals.T[:, :, None]).astype(jnp.bfloat16)

    outputs = lax.map(one_head, (head_queries, head_keys, head_values))
    return outputs.transpose(1, 0, 2, 3).reshape(BLOCK, QHEADS * HD)


def auxiliary_arrays(element_items, border_width, holder_array):
    span_length = element_items[0].shape[0]
    start_displacement = 1
    selected_items = min(span_length, border_width - (start_displacement - 1) * span_length)
    bottom_pieces = [
        holder_array(
            tuple((element_item[span_length - selected_items :] for element_item in element_items)),
            start_displacement,
        )
    ]
    start_displacement = 1
    selected_items = min(span_length, border_width - (start_displacement - 1) * span_length)
    top_pieces = [
        holder_array(
            tuple((element_item[:selected_items] for element_item in element_items)),
            -start_displacement,
        )
    ]
    joined = []
    for column in range(len(element_items)):
        pieces = (
            [part[column] for part in bottom_pieces]
            + [element_items[column]]
            + [part[column] for part in top_pieces]
        )
        joined.append(jnp.concatenate(pieces, axis=0))
    return tuple(joined)


def staying_mask(start_displacement):
    seq_count = lax.axis_size("seq")
    seq_index = lax.axis_index("seq")
    if start_displacement > 0:
        return seq_index >= start_displacement
    return seq_index - start_displacement < seq_count


def token_move(element_items, start_displacement):
    within = jax.tree.map(
        lambda part, own: part.astype(own.dtype),
        shifted(shortened(element_items), "seq", start_displacement),
        element_items,
    )
    across = jax.tree.map(
        lambda part, own: part.astype(own.dtype),
        shifted_2(shortened(within), "outer", 1 if start_displacement > 0 else -1),
        within,
    )
    staying = staying_mask(start_displacement)
    return tuple((jnp.where(staying, first, second) for first, second in zip(within, across)))


def edge_move(element_items, start_displacement):
    return jax.tree.map(
        lambda part, own: part.astype(own.dtype),
        shifted_2(shortened(element_items), "outer", start_displacement),
        element_items,
    )


def group_move(element_items, start_displacement):
    return jax.tree.map(
        lambda part, own: part.astype(own.dtype),
        shifted_2(shortened(element_items), "outer", start_displacement),
        element_items,
    )


def local(queries, keys, values):
    tok_rows = queries.shape[0]
    seq_count = lax.axis_size("seq")
    outer_count = lax.axis_size("outer")
    outer_index = lax.axis_index("outer")
    linear = outer_index * seq_count + lax.axis_index("seq")
    total = tok_rows * seq_count * outer_count
    fine_k, fine_v = auxiliary_arrays((keys, values), BLOCK, token_move)
    fine_start = linear * tok_rows - BLOCK
    pooled_k = pool_level(keys)
    pooled_v = pool_level(values)
    group_k, group_v = sent_together((pooled_k, pooled_v), "seq", 0, 1)
    group_len = group_k.shape[0]
    first_margin = 2 * BLOCK - min(group_len, BLOCK)
    first_k, first_v = auxiliary_arrays((group_k, group_v), first_margin, edge_move)
    first_start = outer_index * group_len - first_margin
    second_k = pool_level(group_k)
    second_v = pool_level(group_v)
    second_len = second_k.shape[0]
    second_margin = 2 * BLOCK - min(second_len, BLOCK)
    middle_k, middle_v = auxiliary_arrays((second_k, second_v), second_margin, group_move)
    middle_start = outer_index * second_len - second_margin
    top_k, top_v = sent_together_2((pool_level(second_k), pool_level(second_v)), "outer", 0, 1)
    top_mask = jnp.ones((top_k.shape[0],), dtype=bool)
    buffers = [
        (fine_k, fine_v, fine_start, total),
        (first_k, first_v, first_start, total // POOL),
        (middle_k, middle_v, middle_start, total // POOL**2),
    ]
    local_blocks = tok_rows // BLOCK

    def one_block(local_block):
        fine_index = linear * local_blocks + local_block
        key_parts = []
        value_parts = []
        mask_parts = []
        for level_index in range(3):
            level_k, level_v, level_start, level_len = buffers[level_index]
            coarse = fine_index // POOL**level_index
            start_row = (coarse - 1) * BLOCK - level_start
            key_parts.append(lax.dynamic_slice_in_dim(level_k, start_row, 3 * BLOCK, 0))
            value_parts.append(lax.dynamic_slice_in_dim(level_v, start_row, 3 * BLOCK, 0))
            positions = (coarse - 1) * BLOCK + jnp.arange(3 * BLOCK, dtype=jnp.int32)
            mask_parts.append((positions >= 0) & (positions < level_len))
        key_parts.append(top_k)
        value_parts.append(top_v)
        mask_parts.append(top_mask)
        query_rows = lax.dynamic_slice_in_dim(queries, local_block * BLOCK, BLOCK, 0)
        return attend_block(
            query_rows,
            jnp.concatenate(key_parts, axis=0),
            jnp.concatenate(value_parts, axis=0),
            jnp.concatenate(mask_parts, axis=0),
        )

    result = lax.map(one_block, jnp.arange(local_blocks, dtype=jnp.int32))
    return result.reshape(tok_rows, QHEADS * HD)


def solution(mesh):
    placed = (P(("outer", "seq"), None), P(("outer", "seq"), None), P(("outer", "seq"), None))
    return jax.shard_map(
        local, mesh=mesh, in_specs=placed, out_specs=P(("outer", "seq"), None), check_vma=False
    )
```

profile of v0, /device:TPU:1, one launch (start us, length us, event | category | flops | bytes accessed | tf_op | source)
XLA Modules:
  0.0 305.0 jit_solution(6162194365010182397)
XLA Ops:
  11.0 9.3 %all-to-all-start = ((bf16[16,64,1024]{2,1,0:T(8,128)(2,1)}), bf16[16,64,1024]{2,1,0:T(8,128)(2,1)S(1)}, u32[]{:S(2)}, u32[]{:S(2)}) async-start(bf16[16,64,1024]{2,1,0:T(8,128)(2,1)} %broadcast_in_dim.41), calls=%async_computation | async-start | bytes 4194304 | tf_op jit(solution)/shard_map/all_to_all | solution.py:41
  21.2 7.2 %collective-permute-start.10 = (bf16[128,512]{0,1:T(8,128)(2,1)S(1)}, bf16[128,512]{0,1:T(8,128)(2,1)S(1)}, u32[]{:S(2)}, u32[]{:S(2)}) collective-permute-start(bf16[128,512]{0,1:T(8,128)(2,1)S(1)} %get-tuple-element.431), channel_id=1, source_target_pairs={{32,0},{64,32},{96,64},{128,96},{160,128},{192,160},{224,192},{256... | collective-permute-start | bytes 393224 | tf_op jit(solution)/shard_map/ppermute | solution.py:24
  32.4 7.3 %collective-permute-start.2 = (bf16[128,512]{0,1:T(8,128)(2,1)}, bf16[128,512]{0,1:T(8,128)(2,1)S(1)}, u32[]{:S(2)}, u32[]{:S(2)}) collective-permute-start(bf16[128,512]{0,1:T(8,128)(2,1)} %get-tuple-element.433), channel_id=1, source_target_pairs={{32,0},{64,32},{96,64},{128,96},{160,128},{192,160},{224,192},{256... | collective-permute-start | bytes 393224 | tf_op jit(solution)/shard_map/ppermute | solution.py:24
  41.6 14.5 %collective-permute-done.10 = bf16[128,512]{0,1:T(8,128)(2,1)S(1)} collective-permute-done((bf16[128,512]{0,1:T(8,128)(2,1)S(1)}, bf16[128,512]{0,1:T(8,128)(2,1)S(1)}, u32[]{:S(2)}, u32[]{:S(2)}) %collective-permute-start.10) | collective-permute-done | bytes 131104 | tf_op jit(solution)/shard_map/ppermute | solution.py:24
  56.1 5.2 %collective-permute-start.11 = (bf16[128,512]{0,1:T(8,128)(2,1)S(1)}, bf16[128,512]{0,1:T(8,128)(2,1)S(1)}, u32[]{:S(2)}, u32[]{:S(2)}) collective-permute-start(bf16[128,512]{0,1:T(8,128)(2,1)S(1)} %collective-permute-done.10), channel_id=1, source_target_pairs={{1,0},{2,1},{3,2},{4,3},{5,4},{6,5},{7,6},{8,7},{9,8},{10,9},{11,1... | collective-permute-start | bytes 393224 | tf_op jit(solution)/shard_map/ppermute | solution.py:30
  61.4 3.1 %collective-permute-done.8 = bf16[128,512]{0,1:T(8,128)(2,1)} collective-permute-done((bf16[128,512]{0,1:T(8,128)(2,1)}, bf16[128,512]{0,1:T(8,128)(2,1)}, u32[]{:S(2)}, u32[]{:S(2)}) %collective-permute-start.8) | collective-permute-done | bytes 131104 | tf_op jit(solution)/shard_map/ppermute | solution.py:24
  64.4 6.8 %collective-permute-start.9 = (bf16[128,512]{0,1:T(8,128)(2,1)}, bf16[128,512]{0,1:T(8,128)(2,1)}, u32[]{:S(2)}, u32[]{:S(2)}) collective-permute-start(bf16[128,512]{0,1:T(8,128)(2,1)} %collective-permute-done.8), channel_id=1, source_target_pairs={{0,1},{1,2},{2,3},{3,4},{4,5},{5,6},{6,7},{7,8},{8,9},{9,10},{10,1... | collective-permute-start | bytes 393224 | tf_op jit(solution)/shard_map/ppermute | solution.py:30
  73.2 3.6 %collective-permute-start.1 = (bf16[128,512]{0,1:T(8,128)(2,1)}, bf16[128,512]{0,1:T(8,128)(2,1)}, u32[]{:S(2)}, u32[]{:S(2)}) collective-permute-start(bf16[128,512]{0,1:T(8,128)(2,1)} %collective-permute-done), channel_id=1, source_target_pairs={{0,1},{1,2},{2,3},{3,4},{4,5},{5,6},{6,7},{7,8},{8,9},{9,10},{10,1... | collective-permute-start | bytes 393224 | tf_op jit(solution)/shard_map/ppermute | solution.py:30
  85.3 3.2 %collective-permute-start.6 = (bf16[128,512]{1,0:T(8,128)(2,1)}, bf16[128,512]{1,0:T(8,128)(2,1)S(1)}, u32[]{:S(2)}, u32[]{:S(2)}) collective-permute-start(bf16[128,512]{1,0:T(8,128)(2,1)} %get-tuple-element.413), channel_id=1, source_target_pairs={{0,1},{1,2},{2,3},{3,4},{4,5},{5,6},{6,7},{7,8},{8,9},{9,10},{10,1... | collective-permute-start | bytes 393224 | tf_op jit(solution)/shard_map/ppermute | solution.py:30
  90.5 3.6 %collective-permute-start.12 = (bf16[128,512]{1,0:T(8,128)(2,1)S(1)}, bf16[128,512]{1,0:T(8,128)(2,1)S(1)}, u32[]{:S(2)}, u32[]{:S(2)}) collective-permute-start(bf16[128,512]{1,0:T(8,128)(2,1)S(1)} %get-tuple-element.422), channel_id=1, source_target_pairs={{0,1},{1,2},{2,3},{3,4},{4,5},{5,6},{6,7},{7,8},{8,9},{9,10},{10,1... | collective-permute-start | bytes 393224 | tf_op jit(solution)/shard_map/ppermute | solution.py:30
  94.2 2.1 collective-permute-start.13
  97.4 3.8 %collective-permute-start.14 = (bf16[128,512]{1,0:T(8,128)(2,1)S(1)}, bf16[128,512]{1,0:T(8,128)(2,1)S(1)}, u32[]{:S(2)}, u32[]{:S(2)}) collective-permute-start(bf16[128,512]{1,0:T(8,128)(2,1)S(1)} %copy-done.6), channel_id=1, source_target_pairs={{0,1},{1,2},{2,3},{3,4},{4,5},{5,6},{6,7},{7,8},{8,9},{9,10},{10,1... | collective-permute-start | bytes 393224 | tf_op jit(solution)/shard_map/ppermute | solution.py:30
  103.1 3.6 %collective-permute-start.4 = (bf16[128,512]{1,0:T(8,128)(2,1)S(1)}, bf16[128,512]{1,0:T(8,128)(2,1)S(1)}, u32[]{:S(2)}, u32[]{:S(2)}) collective-permute-start(bf16[128,512]{1,0:T(8,128)(2,1)S(1)} %get-tuple-element.425), channel_id=1, source_target_pairs={{0,1},{1,2},{2,3},{3,4},{4,5},{5,6},{6,7},{7,8},{8,9},{9,10},{10,1... | collective-permute-start | bytes 393224 | tf_op jit(solution)/shard_map/ppermute | solution.py:30
  111.9 2.4 collective-permute-done.5
  115.5 65.2 %all-gather.2.cloned.1.call-done = bf16[512,1024]{1,0:T(8,128)(2,1)} async-done(((bf16[16,1024]{1,0:T(8,128)(2,1)}), bf16[512,1024]{1,0:T(8,128)(2,1)}) %all-gather.2.cloned.1.call-update) | async-done | bytes 1048592 | tf_op jit(solution)/shard_map/all_gather | solution.py:60
  183.9 114.3 %while.40 = (s32[]{:T(128)}, bf16[4,128,2048]{2,1,0:T(8,128)(2,1)}, s32[4]{0:T(128)S(1)}, bf16[512,2048]{1,0:T(8,128)(2,1)}, s32[]{:T(128)}, /*index=5*/s32[]{:T...) while((s32[]{:T(128)}, bf16[4,128,2048]{2,1,0:T(8,128)(2,1)}, ...), condition=%wide.region_11.12_spmd, body=%wide.region_6.11_spmd.sunk | while | flops 455942560 | bytes 33378624 | solution.py:220
  194.6 2.0 copy.62
  196.7 13.7 %while.41 = (s32[]{:T(128)}, bf16[4,128,4,128]{1,3,2,0:T(8,128)(2,1)}, bf16[4,1664,128]{1,2,0:T(8,128)(2,1)S(1)}, pred[1664]{0:T(1024)(128)(4,1)S(1)}, bf16[4,16...) while((s32[]{:T(128)}, bf16[4,128,4,128]{1,3,2,0:T(8,128)(2,1)}, ...), condition=%wide.region_10.10_spmd, body=%wide.region_7.9_spmd.sunk | while | flops 442301440 | bytes 11352141 | solution.py:93
  223.2 2.0 copy.62
  225.2 13.7 %while.41 = (s32[]{:T(128)}, bf16[4,128,4,128]{1,3,2,0:T(8,128)(2,1)}, bf16[4,1664,128]{1,2,0:T(8,128)(2,1)S(1)}, pred[1664]{0:T(1024)(128)(4,1)S(1)}, bf16[4,16...) while((s32[]{:T(128)}, bf16[4,128,4,128]{1,3,2,0:T(8,128)(2,1)}, ...), condition=%wide.region_10.10_spmd, body=%wide.region_7.9_spmd.sunk | while | flops 442301440 | bytes 11352141 | solution.py:93
  251.8 2.0 copy.62
  253.8 13.7 %while.41 = (s32[]{:T(128)}, bf16[4,128,4,128]{1,3,2,0:T(8,128)(2,1)}, bf16[4,1664,128]{1,2,0:T(8,128)(2,1)S(1)}, pred[1664]{0:T(1024)(128)(4,1)S(1)}, bf16[4,16...) while((s32[]{:T(128)}, bf16[4,128,4,128]{1,3,2,0:T(8,128)(2,1)}, ...), condition=%wide.region_10.10_spmd, body=%wide.region_7.9_spmd.sunk | while | flops 442301440 | bytes 11352141 | solution.py:93
  280.3 2.0 copy.62
  282.4 13.7 %while.41 = (s32[]{:T(128)}, bf16[4,128,4,128]{1,3,2,0:T(8,128)(2,1)}, bf16[4,1664,128]{1,2,0:T(8,128)(2,1)S(1)}, pred[1664]{0:T(1024)(128)(4,1)S(1)}, bf16[4,16...) while((s32[]{:T(128)}, bf16[4,128,4,128]{1,3,2,0:T(8,128)(2,1)}, ...), condition=%wide.region_10.10_spmd, body=%wide.region_7.9_spmd.sunk | while | flops 442301440 | bytes 11352141 | solution.py:93
  (197 shorter events, 137.1 us)
Async XLA Ops:
  11.0 9.4 %copy-start.5 = (bf16[512,512]{1,0:T(8,128)(2,1)S(1)}, bf16[512,512]{1,0:T(8,128)(2,1)}, u32[]{:S(2)}) copy-start(bf16[512,512]{1,0:T(8,128)(2,1)} %param.9) | copy-start | bytes 1572868
  11.0 66.9 %all-to-all-start = ((bf16[16,64,1024]{2,1,0:T(8,128)(2,1)}), bf16[16,64,1024]{2,1,0:T(8,128)(2,1)S(1)}, u32[]{:S(2)}, u32[]{:S(2)}) async-start(bf16[16,64,1024]{2,1,0:T(8,128)(2,1)} %broadcast_in_dim.41), calls=%async_computation | async-start | bytes 4194304 | tf_op jit(solution)/shard_map/all_to_all | solution.py:41
  20.3 160.3 %all-gather.2.cloned.1.call-start = ((), (), s32[]{:S(2)}) async-start(), calls=%async_computation.1 | async-start | bytes 1081344 | tf_op jit(solution)/shard_map/all_gather | solution.py:60
  21.2 34.8 %collective-permute-start.10 = (bf16[128,512]{0,1:T(8,128)(2,1)S(1)}, bf16[128,512]{0,1:T(8,128)(2,1)S(1)}, u32[]{:S(2)}, u32[]{:S(2)}) collective-permute-start(bf16[128,512]{0,1:T(8,128)(2,1)S(1)} %get-tuple-element.431), channel_id=1, source_target_pairs={{32,0},{64,32},{96,64},{128,96},{160,128},{192,160},{224,192},{256... | collective-permute-start | bytes 393224 | tf_op jit(solution)/shard_map/ppermute | solution.py:24
  28.4 36.0 %collective-permute-start.8 = (bf16[128,512]{0,1:T(8,128)(2,1)}, bf16[128,512]{0,1:T(8,128)(2,1)}, u32[]{:S(2)}, u32[]{:S(2)}) collective-permute-start(bf16[128,512]{0,1:T(8,128)(2,1)} %get-tuple-element.430), channel_id=1, source_target_pairs={{480,0},{0,32},{32,64},{64,96},{96,128},{128,160},{160,192},{192,2... | collective-permute-start | bytes 393224 | tf_op jit(solution)/shard_map/ppermute | solution.py:24
  31.6 48.4 %copy-start.3 = (bf16[512,512]{0,1:T(8,128)(2,1)}, bf16[512,512]{0,1:T(8,128)(2,1)S(1)}, u32[]{:S(2)}) copy-start(bf16[512,512]{0,1:T(8,128)(2,1)S(1)} %copy.34) | copy-start | bytes 1572868
  32.4 38.9 %collective-permute-start.2 = (bf16[128,512]{0,1:T(8,128)(2,1)}, bf16[128,512]{0,1:T(8,128)(2,1)S(1)}, u32[]{:S(2)}, u32[]{:S(2)}) collective-permute-start(bf16[128,512]{0,1:T(8,128)(2,1)} %get-tuple-element.433), channel_id=1, source_target_pairs={{32,0},{64,32},{96,64},{128,96},{160,128},{192,160},{224,192},{256... | collective-permute-start | bytes 393224 | tf_op jit(solution)/shard_map/ppermute | solution.py:24
  39.6 33.6 %collective-permute-start = (bf16[128,512]{0,1:T(8,128)(2,1)}, bf16[128,512]{0,1:T(8,128)(2,1)}, u32[]{:S(2)}, u32[]{:S(2)}) collective-permute-start(bf16[128,512]{0,1:T(8,128)(2,1)} %get-tuple-element.432), channel_id=1, source_target_pairs={{480,0},{0,32},{32,64},{64,96},{96,128},{128,160},{160,192},{192,2... | collective-permute-start | bytes 393224 | tf_op jit(solution)/shard_map/ppermute | solution.py:24
  56.1 20.8 %collective-permute-start.11 = (bf16[128,512]{0,1:T(8,128)(2,1)S(1)}, bf16[128,512]{0,1:T(8,128)(2,1)S(1)}, u32[]{:S(2)}, u32[]{:S(2)}) collective-permute-start(bf16[128,512]{0,1:T(8,128)(2,1)S(1)} %collective-permute-done.10), channel_id=1, source_target_pairs={{1,0},{2,1},{3,2},{4,3},{5,4},{6,5},{7,6},{8,7},{9,8},{10,9},{11,1... | collective-permute-start | bytes 393224 | tf_op jit(solution)/shard_map/ppermute | solution.py:30
  64.4 16.9 %collective-permute-start.9 = (bf16[128,512]{0,1:T(8,128)(2,1)}, bf16[128,512]{0,1:T(8,128)(2,1)}, u32[]{:S(2)}, u32[]{:S(2)}) collective-permute-start(bf16[128,512]{0,1:T(8,128)(2,1)} %collective-permute-done.8), channel_id=1, source_target_pairs={{0,1},{1,2},{2,3},{3,4},{4,5},{5,6},{6,7},{7,8},{8,9},{9,10},{10,1... | collective-permute-start | bytes 393224 | tf_op jit(solution)/shard_map/ppermute | solution.py:30
  71.3 6.6 %collective-permute-start.3 = (bf16[128,512]{0,1:T(8,128)(2,1)S(1)}, bf16[128,512]{0,1:T(8,128)(2,1)S(1)}, u32[]{:S(2)}, u32[]{:S(2)}) collective-permute-start(bf16[128,512]{0,1:T(8,128)(2,1)S(1)} %collective-permute-done.2), channel_id=1, source_target_pairs={{1,0},{2,1},{3,2},{4,3},{5,4},{6,5},{7,6},{8,7},{9,8},{10,9},{11,1... | collective-permute-start | bytes 393224 | tf_op jit(solution)/shard_map/ppermute | solution.py:30
  73.2 10.1 %collective-permute-start.1 = (bf16[128,512]{0,1:T(8,128)(2,1)}, bf16[128,512]{0,1:T(8,128)(2,1)}, u32[]{:S(2)}, u32[]{:S(2)}) collective-permute-start(bf16[128,512]{0,1:T(8,128)(2,1)} %collective-permute-done), channel_id=1, source_target_pairs={{0,1},{1,2},{2,3},{3,4},{4,5},{5,6},{6,7},{7,8},{8,9},{9,10},{10,1... | collective-permute-start | bytes 393224 | tf_op jit(solution)/shard_map/ppermute | solution.py:30
  85.3 22.6 %collective-permute-start.6 = (bf16[128,512]{1,0:T(8,128)(2,1)}, bf16[128,512]{1,0:T(8,128)(2,1)S(1)}, u32[]{:S(2)}, u32[]{:S(2)}) collective-permute-start(bf16[128,512]{1,0:T(8,128)(2,1)} %get-tuple-element.413), channel_id=1, source_target_pairs={{0,1},{1,2},{2,3},{3,4},{4,5},{5,6},{6,7},{7,8},{8,9},{9,10},{10,1... | collective-permute-start | bytes 393224 | tf_op jit(solution)/shard_map/ppermute | solution.py:30
  88.5 21.4 %collective-permute-start.7 = (bf16[128,512]{1,0:T(8,128)(2,1)}, bf16[128,512]{1,0:T(8,128)(2,1)S(1)}, u32[]{:S(2)}, u32[]{:S(2)}) collective-permute-start(bf16[128,512]{1,0:T(8,128)(2,1)} %get-tuple-element.413), channel_id=1, source_target_pairs={{1,0},{2,1},{3,2},{4,3},{5,4},{6,5},{7,6},{8,7},{9,8},{10,9},{11,1... | collective-permute-start | bytes 393224 | tf_op jit(solution)/shard_map/ppermute | solution.py:30
  90.5 10.7 %collective-permute-start.12 = (bf16[128,512]{1,0:T(8,128)(2,1)S(1)}, bf16[128,512]{1,0:T(8,128)(2,1)S(1)}, u32[]{:S(2)}, u32[]{:S(2)}) collective-permute-start(bf16[128,512]{1,0:T(8,128)(2,1)S(1)} %get-tuple-element.422), channel_id=1, source_target_pairs={{0,1},{1,2},{2,3},{3,4},{4,5},{5,6},{6,7},{7,8},{8,9},{9,10},{10,1... | collective-permute-start | bytes 393224 | tf_op jit(solution)/shard_map/ppermute | solution.py:30
  94.2 8.9 %collective-permute-start.13 = (bf16[128,512]{1,0:T(8,128)(2,1)S(1)}, bf16[128,512]{1,0:T(8,128)(2,1)S(1)}, u32[]{:S(2)}, u32[]{:S(2)}) collective-permute-start(bf16[128,512]{1,0:T(8,128)(2,1)S(1)} %get-tuple-element.423), channel_id=1, source_target_pairs={{1,0},{2,1},{3,2},{4,3},{5,4},{6,5},{7,6},{8,7},{9,8},{10,9},{11,1... | collective-permute-start | bytes 393224 | tf_op jit(solution)/shard_map/ppermute | solution.py:30
  97.4 12.6 %copy-start.7 = (bf16[128,512]{1,0:T(8,128)(2,1)S(1)}, bf16[128,512]{1,0:T(8,128)(2,1)}, u32[]{:S(2)}) copy-start(bf16[128,512]{1,0:T(8,128)(2,1)} %get-tuple-element.413) | copy-start | bytes 393220
  97.4 13.6 %collective-permute-start.14 = (bf16[128,512]{1,0:T(8,128)(2,1)S(1)}, bf16[128,512]{1,0:T(8,128)(2,1)S(1)}, u32[]{:S(2)}, u32[]{:S(2)}) collective-permute-start(bf16[128,512]{1,0:T(8,128)(2,1)S(1)} %copy-done.6), channel_id=1, source_target_pairs={{0,1},{1,2},{2,3},{3,4},{4,5},{5,6},{6,7},{7,8},{8,9},{9,10},{10,1... | collective-permute-start | bytes 393224 | tf_op jit(solution)/shard_map/ppermute | solution.py:30
  101.2 9.8 %collective-permute-start.15 = (bf16[128,512]{1,0:T(8,128)(2,1)S(1)}, bf16[128,512]{1,0:T(8,128)(2,1)S(1)}, u32[]{:S(2)}, u32[]{:S(2)}) collective-permute-start(bf16[128,512]{1,0:T(8,128)(2,1)S(1)} %copy-done.6), channel_id=1, source_target_pairs={{1,0},{2,1},{3,2},{4,3},{5,4},{6,5},{7,6},{8,7},{9,8},{10,9},{11,1... | collective-permute-start | bytes 393224 | tf_op jit(solution)/shard_map/ppermute | solution.py:30
  103.1 8.8 %collective-permute-start.4 = (bf16[128,512]{1,0:T(8,128)(2,1)S(1)}, bf16[128,512]{1,0:T(8,128)(2,1)S(1)}, u32[]{:S(2)}, u32[]{:S(2)}) collective-permute-start(bf16[128,512]{1,0:T(8,128)(2,1)S(1)} %get-tuple-element.425), channel_id=1, source_target_pairs={{0,1},{1,2},{2,3},{3,4},{4,5},{5,6},{6,7},{7,8},{8,9},{9,10},{10,1... | collective-permute-start | bytes 393224 | tf_op jit(solution)/shard_map/ppermute | solution.py:30
  107.9 6.4 %copy-start.2 = (bf16[1024,512]{1,0:T(8,128)(2,1)S(1)}, bf16[1024,512]{1,0:T(8,128)(2,1)}, u32[]{:S(2)}) copy-start(bf16[1024,512]{1,0:T(8,128)(2,1)} %get-tuple-element.427) | copy-start | bytes 3145732
  107.9 6.4 %collective-permute-start.5 = (bf16[128,512]{1,0:T(8,128)(2,1)S(1)}, bf16[128,512]{1,0:T(8,128)(2,1)S(1)}, u32[]{:S(2)}, u32[]{:S(2)}) collective-permute-start(bf16[128,512]{1,0:T(8,128)(2,1)S(1)} %get-tuple-element.424), channel_id=1, source_target_pairs={{1,0},{2,1},{3,2},{4,3},{5,4},{6,5},{7,6},{8,7},{9,8},{10,9},{11,1... | collective-permute-start | bytes 393224 | tf_op jit(solution)/shard_map/ppermute | solution.py:30
  212.5 6.2 %copy-start = (bf16[768,512]{0,1:T(8,128)(2,1)}, bf16[768,512]{0,1:T(8,128)(2,1)S(1)}, u32[]{:S(2)}) copy-start(bf16[768,512]{0,1:T(8,128)(2,1)S(1)} %get-tuple-element.677) | copy-start | bytes 2359300 | tf_op jit(solution)/shard_map/while
  241.1 6.2 %copy-start = (bf16[768,512]{0,1:T(8,128)(2,1)}, bf16[768,512]{0,1:T(8,128)(2,1)S(1)}, u32[]{:S(2)}) copy-start(bf16[768,512]{0,1:T(8,128)(2,1)S(1)} %get-tuple-element.677) | copy-start | bytes 2359300 | tf_op jit(solution)/shard_map/while
  (8 other events, 27.3 us)
Sparse Core Ops, SparseCore 0:
  81.5 99.0 all-gather.1
where the time goes:
time: 307 us; the launch traced here: 305 us
  waiting for transfers between devices  85.5 us (28%)
  starting transfers between devices  67.5 us (22%)
  local copies, waits for them, and re-layouts  57.8 us (19%)
  matrix products  47.1 us (15%)
  other arithmetic  28.4 us (9%)
  between operations  13.8 us (4%)
  loops' own time  5.06 us (2%)
    all_gather x1, waiting for transfers between devices, sent_together_2(): result = lax.all_gather(both, axis, axis=dim, tiled=True)  65.2 us
    ppermute x12, starting transfers between devices, shifted_2(): lax.ppermute(value, axis, [(source, source + steps) for source in range(f...  39.8 us
    dot_general x16, matrix products, one_head(): jnp.einsum('tgd,sd->gts', part_q, part_k, preferred_element_type=jnp.floa...  24.9 us
    dot_general x16, matrix products, one_head(): jnp.einsum('gts,sd->tgd', rounded, part_v, preferred_element_type=jnp.flo...  22.1 us
    ppermute x4, starting transfers between devices, shifted(): return lax.ppermute(block, axis, route)  18.3 us
    ppermute x4, waiting for transfers between devices, shifted(): return lax.ppermute(block, axis, route)  17.6 us
    dynamic_slice x8, local copies, waits for them, and re-layouts, one_block(): lax.dynamic_slice_in_dim(queries, local_block * BLOCK, BLOCK, 0)  15.8 us
    dynamic_slice x12, local copies, waits for them, and re-layouts, one_block(): key_parts.append(lax.dynamic_slice_in_dim(level_k, start_row, 3 * BLOCK, 0))  12 us
  transfers between devices with their start and end apart: 18, of which 5 were waited for; matrix products, arithmetic and copies ran while one was open for 5% of the time, Pallas kernels for 0%

commit v1 on v0

v1 whole, which is shorter than its diff:
```python
import functools

import jax
import jax.numpy as jnp
from jax import lax
from jax.experimental import pallas as pl
from jax.experimental.pallas import tpu as pltpu
from jax.sharding import Mesh
from jax.sharding import PartitionSpec as P


HD = 128
QHEADS = 16
KVHEADS = 4
GROUP = QHEADS // KVHEADS
BLOCK = 128
POOL = 8
WIDTH = KVHEADS * HD
TILE = 256
SCALE = HD ** (-0.5) * 1.4426950408889634
FINE = ("y", "z_lo", "z_hi", "x", "core")
TOKEN_ORDER = ("z_hi", "x", "core", "y", "z_lo")
SEQ, OUTER = 16, 32
VMEM = 67043328
COUNT = SEQ * OUTER


def holds(flags, bit):
    return (flags[0] >> bit) % 2 == 1


def pooling_matrix(rows):
    first = lax.broadcasted_iota(jnp.int32, (rows // POOL, rows), 0)
    second = lax.broadcasted_iota(jnp.int32, (rows // POOL, rows), 1)
    return jnp.where(second // POOL == first, 1.0, 0.0).astype(jnp.bfloat16)


def pooled(rows):
    summed = jnp.dot(pooling_matrix(rows.shape[0]), rows, preferred_element_type=jnp.float32)
    return (summed * POOL ** (-0.5)).astype(jnp.bfloat16)


def pool_kernel(flags, k_ref, v_ref, first_ref, second_ref, partner_ref, other_ref):
    rows = k_ref.shape[0]
    odd = holds(flags, 5)
    for part, ref in enumerate((k_ref, v_ref)):
        columns = slice(part * WIDTH, (part + 1) * WIDTH)
        one = pooled(ref[...])
        first_ref[:, columns] = one
        partner_ref[BLOCK:, columns] = one
        other_ref[BLOCK:, columns] = one
        two = pooled(one)
        for copy in range(second_ref.shape[0]):
            second_ref[copy, :, columns] = two

        @pl.when(odd)
        def _():
            partner_ref[:BLOCK, columns] = ref[:BLOCK]
            other_ref[:BLOCK, columns] = ref[rows - BLOCK :]

        @pl.when(jnp.logical_not(odd))
        def _():
            partner_ref[:BLOCK, columns] = ref[rows - BLOCK :]
            other_ref[:BLOCK, columns] = ref[:BLOCK]


def pool_local(flags, keys, values):
    first = keys.shape[0] // POOL
    shapes = [(first,), (SEQ, first // POOL), (BLOCK + first,), (BLOCK + first,)]
    vmem = pl.BlockSpec(memory_space=pltpu.VMEM)
    return pl.pallas_call(
        pool_kernel,
        in_specs=[pl.BlockSpec(memory_space=pltpu.SMEM), vmem, vmem],
        out_shape=[jax.ShapeDtypeStruct((*n, 2 * WIDTH), jnp.bfloat16) for n in shapes],
        compiler_params=pltpu.CompilerParams(vmem_limit_bytes=VMEM),
        name="pool_local",
    )(flags, keys, values)


def pool_again_kernel(rows_ref, out_ref):
    rows = pooled(rows_ref[...])
    for copy in range(out_ref.shape[0]):
        out_ref[copy] = rows


def pool_again(rows, copies):
    return pl.pallas_call(
        pool_again_kernel,
        out_shape=jax.ShapeDtypeStruct((copies, rows.shape[0] // POOL, rows.shape[1]), jnp.bfloat16),
        compiler_params=pltpu.CompilerParams(vmem_limit_bytes=VMEM),
        name="pool_again",
    )(rows)


def chunks_of(windows):
    tiles, tile, room = [], [], TILE
    for start, length in windows:
        while length:
            take = min(room, length)
            tile.append((start, take))
            start, length, room = start + take, length - take, room - take
            if room == 0:
                tiles.append(tile)
                tile, room = [], TILE
    if tile:
        tiles.append(tile)
    return tiles


def rows_of(ref, tile):
    parts = [ref[start : start + length, :] for start, length in tile]
    return parts[0] if len(parts) == 1 else jnp.concatenate(parts, axis=0)


def attend_kernel(count, pieces, swaps, guards, windows, earlier, later, *refs):
    refs = list(refs)
    flags = refs.pop(0)
    q_ref = refs.pop(0)
    sources = [(refs.pop(0), refs.pop(0)) for _ in range(count)]
    before = (refs.pop(0), refs.pop(0)) if earlier else None
    o_ref = refs.pop(0)
    lse_ref = refs.pop(0) if later else None
    kx, vx, s_ref, p_ref, m_ref = refs
    places, held = [], 0
    for _, _, rows in pieces:
        places.append(held)
        held += rows

    def fill(piece, taken):
        source, first, rows = pieces[taken]
        here = slice(places[piece], places[piece] + rows)
        kx[here, :] = sources[source][0][first : first + rows, :]
        vx[here, :HD] = sources[source][1][first : first + rows, :]

    vx[:, HD:] = jnp.ones((held, HD), jnp.bfloat16)
    for piece in range(len(pieces)):
        if piece not in swaps:
            fill(piece, piece)
    for order, wanted in ((swaps, False), (swaps[::-1], True)) if swaps else ():

        @pl.when(holds(flags, 5) == wanted)
        def _():
            for piece, taken in zip(swaps, order):
                fill(piece, taken)

    for piece, (flag, stand_in) in guards.items():
        rows = pieces[piece][2]
        here = slice(places[piece], places[piece] + rows)

        @pl.when(jnp.logical_not(holds(flags, flag)))
        def _():
            kx[here, :] = kx[places[stand_in] : places[stand_in] + rows, :]
            vx[here, :] = jnp.zeros((rows, 2 * HD), jnp.bfloat16)

    blocks = q_ref.shape[0] // BLOCK
    rows = GROUP * BLOCK
    step = 32

    def score(b):
        slot = b % 2
        q4 = jnp.concatenate(
            [q_ref[b * BLOCK : (b + 1) * BLOCK, g * HD : (g + 1) * HD] for g in range(GROUP)], axis=0
        )
        at = 0
        for tile in chunks_of(windows(b)):
            part = rows_of(kx, tile)
            s_ref[slot, :, at : at + part.shape[0]] = lax.dot_general(
                q4, part, (((1,), (1,)), ((), ())), preferred_element_type=jnp.float32
            )
            at += part.shape[0]
        for r in range(0, rows, step):
            here = slice(r, r + step)
            top = jnp.max(s_ref[slot, here, :], axis=1, keepdims=True) * SCALE
            top = jnp.broadcast_to(top, (step, HD))
            if earlier:
                top = jnp.maximum(top, before[1][b * rows + r : b * rows + r + step, :])
            m_ref[slot, here, :] = top

    def finish(b):
        slot = b % 2
        width = s_ref.shape[2]
        for r in range(0, rows, step):
            here = slice(r, r + step)
            top = m_ref[slot, here, :]
            for a in range(0, width, HD):
                weight = jnp.exp2(s_ref[slot, here, a : a + HD] * SCALE - top)
                p_ref[slot, here, a : a + HD] = weight.astype(jnp.bfloat16)
        total = None
        at = 0
        for tile in chunks_of(windows(b)):
            part = rows_of(vx, tile)
            mixed = jnp.dot(
                p_ref[slot, :, at : at + part.shape[0]], part, preferred_element_type=jnp.float32
            )
            total = mixed if total is None else total + mixed
            at += part.shape[0]
        for g in range(GROUP):
            head = slice(g * BLOCK, (g + 1) * BLOCK)
            tokens = slice(b * BLOCK, (b + 1) * BLOCK)
            columns = slice(g * HD, (g + 1) * HD)
            upper, lower = total[head, :HD], total[head, HD:]
            if earlier:
                place = slice(b * rows + g * BLOCK, b * rows + (g + 1) * BLOCK)
                share = jnp.exp2(before[1][place, :] - m_ref[slot, head, :])
                upper = upper + share * before[0][tokens, columns].astype(jnp.float32)
                lower = lower + share
            o_ref[tokens, columns] = (upper / lower).astype(o_ref.dtype)
            if later:
                place = slice(b * rows + g * BLOCK, b * rows + (g + 1) * BLOCK)
                lse_ref[place, :] = m_ref[slot, head, :] + jnp.log2(lower)

    score(0)
    for b in range(blocks):
        if b + 1 < blocks:
            score(b + 1)
        finish(b)


def attend(flags, queries, sources, pieces, swaps, guards, windows, width, before=None, later=False):
    tokens = queries.shape[0]
    rows = tokens * GROUP
    held = sum(n for _, _, n in pieces)
    wide = pl.BlockSpec((tokens, GROUP * HD), lambda h: (0, h))
    tall = pl.BlockSpec((rows, HD), lambda h: (h, 0))

    def narrow(array, offset):
        return pl.BlockSpec((array.shape[0], HD), lambda h: (0, h + offset))

    in_specs = [pl.BlockSpec(memory_space=pltpu.SMEM), wide]
    operands = [flags, queries]
    for k, k_at, v, v_at in sources:
        in_specs += [narrow(k, k_at), narrow(v, v_at)]
        operands += [k, v]
    if before is not None:
        in_specs += [wide, tall]
        operands += list(before)
    out_shape = [jax.ShapeDtypeStruct(queries.shape, jnp.bfloat16)]
    out_specs = [wide]
    if later:
        out_shape.append(jax.ShapeDtypeStruct((KVHEADS * rows, HD), jnp.float32))
        out_specs.append(tall)
    unit = GROUP * BLOCK
    return pl.pallas_call(
        functools.partial(
            attend_kernel, len(sources), pieces, swaps, guards, windows, before is not None, later
        ),
        grid=(KVHEADS,),
        in_specs=in_specs,
        out_specs=out_specs,
        out_shape=out_shape,
        scratch_shapes=[
            pltpu.VMEM((held, HD), jnp.bfloat16),
            pltpu.VMEM((held, 2 * HD), jnp.bfloat16),
            pltpu.VMEM((2, unit, width), jnp.float32),
            pltpu.VMEM((2, unit, width), jnp.bfloat16),
            pltpu.VMEM((2, unit, HD), jnp.float32),
        ],
        compiler_params=pltpu.CompilerParams(
            dimension_semantics=("arbitrary",), vmem_limit_bytes=VMEM
        ),
        cost_estimate=pl.CostEstimate(
            flops=4 * tokens * QHEADS * HD * width,
            bytes_accessed=6 * tokens * QHEADS * HD,
            transcendentals=tokens * QHEADS * width,
        ),
    )(*operands)


def placed_at(token_index):
    return (token_index % SEQ) * OUTER + token_index // SEQ


def moved(rows, source_of):
    route = [
        (placed_at(source_of(i)), placed_at(i)) for i in range(COUNT) if 0 <= source_of(i) < COUNT
    ]
    return lax.ppermute(rows, FINE, route)


def exchanged(copies, axis):
    result = lax.all_to_all(copies, axis, 0, 0, tiled=True)
    return result.reshape(-1, result.shape[-1])


def one_device(queries, keys, values):
    outer = (lax.axis_index("z_hi") * 4 + lax.axis_index("x")) * 2 + lax.axis_index("core")
    index = outer * SEQ + lax.axis_index("y") * 4 + lax.axis_index("z_lo")
    flags = [
        index > 0,
        index < COUNT - 1,
        (index >= 2) & (index < COUNT - 2),
        (outer > 0) & (outer < OUTER - 1),
        (index > 0) & (index < COUNT - 1),
        index % 2,
        (index != 1) & (index != COUNT - 2),
    ]
    flags = sum(jnp.asarray(e, jnp.int32) << k for k, e in enumerate(flags)).reshape(1)

    first, second, to_partner, to_other = pool_local(flags, keys, values)

    group = exchanged(second, ("y", "z_lo"))
    partner = moved(to_partner, lambda i: i ^ 1)
    other = moved(to_other, lambda i: i + 1 if i % 2 else i - 1)
    two = moved(first, lambda i: i ^ 2)
    third = moved(first, lambda i: i - 3 if i % 2 else i + 3)
    far = moved(first, lambda i: i - 2 if i % 4 < 2 else i + 2)

    top = exchanged(pool_again(group, 4), "z_hi")
    top = exchanged(jnp.broadcast_to(top[None], (4, *top.shape)), "x")
    group_pair = moved(group, lambda i: i ^ SEQ)
    group_other = moved(group, lambda i: i + SEQ if (i // SEQ) % 2 else i - SEQ)
    top_pair = moved(top, lambda i: i ^ SEQ)

    def both(array):
        return (array, 0, array, KVHEADS)

    def whole(arrays):
        return [(k, 0, array[0].shape[0]) for k, array in enumerate(arrays)]

    rows = keys.shape[0]
    firsts = first.shape[0]
    near = [(keys, 0, values, 0)] + [both(a) for a in (other, partner, first, two, third, far)]
    pieces = [(1, 0, BLOCK), (0, 0, rows), (2, 0, BLOCK), (3, 0, firsts), (2, BLOCK, firsts)]
    pieces += [(1, BLOCK, firsts), (4, 0, firsts), (5, 0, firsts), (6, 0, firsts)]
    part, lse = attend(
        flags,
        queries,
        near,
        pieces,
        [0, 2],
        {0: (0, 1), 2: (1, 1), 5: (4, 3), 7: (6, 3), 8: (2, 3)},
        lambda b: [(b * BLOCK, 3 * BLOCK), (rows + 2 * BLOCK, 3 * BLOCK)],
        6 * BLOCK,
        later=True,
    )
    coarse = [both(a) for a in (top, top_pair, group, group_pair, group_other)]
    tops = 2 * top.shape[0]
    (out,) = attend(
        flags,
        queries,
        coarse,
        whole(coarse),
        [],
        {4: (3, 2)},
        lambda b: [(0, tops + 3 * BLOCK)],
        tops + 3 * BLOCK,
        before=(part, lse),
    )
    return out


def solution(mesh):
    assert mesh.axis_names == ("seq", "outer")
    split = Mesh(mesh.devices.reshape(4, 4, 4, 4, 2), FINE)
    placed = P(TOKEN_ORDER, None)
    return jax.shard_map(
        one_device, mesh=split, in_specs=(placed,) * 3, out_specs=placed, check_vma=False
    )
```

time: 307 us -> 127 us (0.41)
  the two profiles are of different devices: /device:TPU:1 before, /device:TPU:111 now
where the time goes in v1:
time: 127 us; the launch traced here: 126 us
  starting transfers between devices  46.8 us (37%)
  blocking collectives  38.2 us (30%)
  Pallas kernels  34.2 us (27%)
  waiting for transfers between devices  5.88 us (5%)
    ppermute x8, starting transfers between devices, moved(): return lax.ppermute(rows, FINE, route)  42.5 us
    all_to_all x2, blocking collectives, exchanged(): result = lax.all_to_all(copies, axis, 0, 0, tiled=True)  38.2 us
    pallas_call x2, Pallas kernels, attend(): pl.pallas_call(functools.partial(attend_kernel, len(sources), pieces, swa...  29.5 us
    ppermute x8, waiting for transfers between devices, moved(): return lax.ppermute(rows, FINE, route)  5.88 us
    all_to_all x1, starting transfers between devices, exchanged(): result = lax.all_to_all(copies, axis, 0, 0, tiled=True)  4.29 us
    pallas_call x1, Pallas kernels, pool_local(): pl.pallas_call(pool_kernel, in_specs=[pl.BlockSpec(memory_space=pltpu.SME...  2.9 us
  transfers between devices with their start and end apart: 9, of which 1 were waited for; matrix products, arithmetic and copies ran while one was open for 0% of the time, Pallas kernels for 11%

profile of v1, /device:TPU:111, one launch (start us, length us, event | category | flops | bytes accessed | tf_op | source)
XLA Modules:
  0.0 126.1 jit_solution(8317159803921370888)
XLA Ops:
  0.0 2.9 %pool_local.1 = (bf16[64,1024]{1,0:T(8,128)(2,1)}, bf16[16,8,1024]{2,1,0:T(8,128)(2,1)}, bf16[192,1024]{1,0:T(8,128)(2,1)}, bf16[192,1024]{1,0:T(8,128)(2,1)}) custom-call(s32[1]{0:T(128)} %bitcast.flags.refs_0_, bf16[512,512]{1,0:T(8,128)(2,1)} %refs_2_.1, bf16[512,512]{1,0:T(8,128)(2,1)} %refs_3_.1), custom_call_target="tpu_custom_call" | custom-call | tf_op jit(solution)/shard_map/pool_local/pallas_call | solution.py:71
  2.9 14.0 %all_to_all.15 = bf16[16,8,1024]{2,1,0:T(8,128)(2,1)} all-to-all(bf16[16,8,1024]{2,1,0:T(8,128)(2,1)} %get-tuple-element.11), channel_id=1, replica_groups=mesh['y'=4,'z_lo'=4,'z_hi'=4,'x'=4,'core'=2] {'y','z_lo'}, dimensions={0} | all-to-all | bytes 524288 | tf_op jit(solution)/shard_map/all_to_all | solution.py:281
  16.9 1.8 %pool_again.1 = bf16[4,16,1024]{2,1,0:T(8,128)(2,1)} custom-call(bf16[128,1024]{1,0:T(8,128)(2,1)} %bitcast.4), custom_call_target="tpu_custom_call" | custom-call | tf_op jit(solution)/shard_map/pool_again/pallas_call | solution.py:87
  18.6 24.3 %all_to_all.16 = bf16[4,16,1024]{2,1,0:T(8,128)(2,1)S(1)} all-to-all(bf16[4,16,1024]{2,1,0:T(8,128)(2,1)} %pool_again.1), channel_id=1, replica_groups=mesh['y'=4,'z_lo'=4,'z_hi'=4,'x'=4,'core'=2] {'z_hi'}, dimensions={0} | all-to-all | bytes 262144 | tf_op jit(solution)/shard_map/all_to_all | solution.py:281
  42.9 0.9 broadcast_in_dim.8
  43.8 4.3 %all-to-all-start.2 = ((bf16[4,64,1024]{2,1,0:T(8,128)(2,1)}), bf16[4,64,1024]{2,1,0:T(8,128)(2,1)}, u32[]{:S(2)}, u32[]{:S(2)}) async-start(bf16[4,64,1024]{2,1,0:T(8,128)(2,1)} %broadcast_in_dim.8), calls=%async_computation.2 | async-start | bytes 1048576 | tf_op jit(solution)/shard_map/all_to_all | solution.py:281
  48.1 4.0 %collective-permute-start.3 = (bf16[192,1024]{1,0:T(8,128)(2,1)}, bf16[192,1024]{1,0:T(8,128)(2,1)}, u32[]{:S(2)}, u32[]{:S(2)}) collective-permute-start(bf16[192,1024]{1,0:T(8,128)(2,1)} %get-tuple-element.12), channel_id=1, source_target_pairs={{64,32},{32,64},{128,96},{96,128},{192,160},{160,192},{256,224},{2... | collective-permute-start | bytes 1179656 | tf_op jit(solution)/shard_map/ppermute | solution.py:277
  52.0 1.9 %collective-permute-start.4 = (bf16[192,1024]{1,0:T(8,128)(2,1)}, bf16[192,1024]{1,0:T(8,128)(2,1)}, u32[]{:S(2)}, u32[]{:S(2)}) collective-permute-start(bf16[192,1024]{1,0:T(8,128)(2,1)} %get-tuple-element.13), channel_id=1, source_target_pairs={{32,0},{0,32},{96,64},{64,96},{160,128},{128,160},{224,192},{192,2... | collective-permute-start | bytes 1179656 | tf_op jit(solution)/shard_map/ppermute | solution.py:277
  54.0 4.3 %collective-permute-start.7 = (bf16[64,1024]{1,0:T(8,128)(2,1)}, bf16[64,1024]{1,0:T(8,128)(2,1)}, u32[]{:S(2)}, u32[]{:S(2)}) collective-permute-start(bf16[64,1024]{1,0:T(8,128)(2,1)} %get-tuple-element.14.refs_8_.refs_9_), channel_id=1, source_target_pairs={{128,64},{160,96},{64,128},{96,160},{256,192},{288,224},{192,256},... | collective-permute-start | bytes 393224 | tf_op jit(solution)/shard_map/ppermute | solution.py:277
  58.2 0.0 all-to-all-done.2
  58.2 7.3 %collective-permute-start = (bf16[256,1024]{1,0:T(8,128)(2,1)}, bf16[256,1024]{1,0:T(8,128)(2,1)}, u32[]{:S(2)}, u32[]{:S(2)}) collective-permute-start(bf16[256,1024]{1,0:T(8,128)(2,1)} %bitcast.3.refs_2_.refs_3_), channel_id=1, source_target_pairs={{1,0},{33,32},{65,64},{97,96},{129,128},{161,160},{193,192},{225,2... | collective-permute-start | bytes 1572872 | tf_op jit(solution)/shard_map/ppermute | solution.py:277
  65.6 2.4 %collective-permute-start.6 = (bf16[64,1024]{1,0:T(8,128)(2,1)}, bf16[64,1024]{1,0:T(8,128)(2,1)}, u32[]{:S(2)}, u32[]{:S(2)}) collective-permute-start(bf16[64,1024]{1,0:T(8,128)(2,1)} %get-tuple-element.14.refs_8_.refs_9_), channel_id=1, source_target_pairs={{96,0},{160,64},{0,96},{224,128},{64,160},{288,192},{128,224},{352... | collective-permute-start | bytes 393224 | tf_op jit(solution)/shard_map/ppermute | solution.py:277
  68.0 5.9 %collective-permute-done.7.refs_14_.refs_15_ = bf16[64,1024]{1,0:T(8,128)(2,1)} collective-permute-done((bf16[64,1024]{1,0:T(8,128)(2,1)}, bf16[64,1024]{1,0:T(8,128)(2,1)}, u32[]{:S(2)}, u32[]{:S(2)}) %collective-permute-start.7) | collective-permute-done | bytes 131104 | tf_op jit(solution)/shard_map/ppermute | solution.py:277
  73.8 3.0 %collective-permute-start.5 = (bf16[64,1024]{1,0:T(8,128)(2,1)}, bf16[64,1024]{1,0:T(8,128)(2,1)}, u32[]{:S(2)}, u32[]{:S(2)}) collective-permute-start(bf16[64,1024]{1,0:T(8,128)(2,1)} %get-tuple-element.14.refs_8_.refs_9_), channel_id=1, source_target_pairs={{64,0},{96,32},{0,64},{32,96},{192,128},{224,160},{128,192},{160,2... | collective-permute-start | bytes 393224 | tf_op jit(solution)/shard_map/ppermute | solution.py:277
  76.8 0.0 collective-permute-done.6.refs_12_.refs_13_
  76.8 8.5 %collective-permute-start.2 = (bf16[128,1024]{1,0:T(8,128)(2,1)}, bf16[128,1024]{1,0:T(8,128)(2,1)}, u32[]{:S(2)}, u32[]{:S(2)}) collective-permute-start(bf16[128,1024]{1,0:T(8,128)(2,1)} %bitcast.5), channel_id=1, source_target_pairs={{2,1},{34,33},{66,65},{98,97},{130,129},{162,161},{194,193},{226,2... | collective-permute-start | bytes 786440 | tf_op jit(solution)/shard_map/ppermute | solution.py:277
  85.3 0.0 collective-permute-done.5.refs_10_.refs_11_
  85.3 11.2 %collective-permute-start.1 = (bf16[128,1024]{1,0:T(8,128)(2,1)}, bf16[128,1024]{1,0:T(8,128)(2,1)}, u32[]{:S(2)}, u32[]{:S(2)}) collective-permute-start(bf16[128,1024]{1,0:T(8,128)(2,1)} %bitcast.6), channel_id=1, source_target_pairs={{1,0},{33,32},{65,64},{97,96},{129,128},{161,160},{193,192},{225,2... | collective-permute-start | bytes 786440 | tf_op jit(solution)/shard_map/ppermute | solution.py:277
  96.5 0.0 collective-permute-done.3.refs_4_.refs_5_
  96.5 0.0 collective-permute-done.4.refs_6_.refs_7_
  96.5 13.8 %shard_map.37 = (bf16[512,2048]{1,0:T(8,128)(2,1)}, f32[8192,128]{1,0:T(8,128)}) custom-call(s32[1]{0:T(128)} %bitcast.flags.refs_0_, bf16[512,2048]{1,0:T(8,128)(2,1)} %refs_1_.3, bf16[512,512]{1,0:T(8,128)(2,1)} %refs_2_.1, bf16[512,512]{1,0:T(8,128)(2,1)} %refs_3_.1, bf16[192,1024]{1,0:T(8,128)(2,1)} %collective-permute-done.3.refs_4_.refs_5_, ...), custom_call_target="tpu_custom_call" | custom-call | flops 3221225472 | bytes 6291456 | tf_op jit(solution)/shard_map/pallas_call | solution.py:243
  110.3 0.0 collective-permute-done.2.refs_10_.refs_11_
  110.3 0.0 collective-permute-done.refs_4_.refs_5_
  110.3 15.7 %shard_map.38 = bf16[512,2048]{1,0:T(8,128)(2,1)} custom-call(s32[1]{0:T(128)} %bitcast.flags.refs_0_, bf16[512,2048]{1,0:T(8,128)(2,1)} %refs_1_.3, bf16[256,1024]{1,0:T(8,128)(2,1)} %bitcast.3.refs_2_.refs_3_, bf16[256,1024]{1,0:T(8,128)(2,1)} %bitcast.3.refs_2_.refs_3_, bf16[256,1024]{1,0:T(8,128)(2,1)} %collective-permute-done.refs_4_.refs_5_, ...), custom_call_target="tpu_custom_call" | custom-call | flops 3758096384 | bytes 6291456 | tf_op jit(solution)/shard_map/pallas_call | solution.py:243
  (1 shorter events, 0.0 us)
Async XLA Ops:
  43.8 14.5 %all-to-all-start.2 = ((bf16[4,64,1024]{2,1,0:T(8,128)(2,1)}), bf16[4,64,1024]{2,1,0:T(8,128)(2,1)}, u32[]{:S(2)}, u32[]{:S(2)}) async-start(bf16[4,64,1024]{2,1,0:T(8,128)(2,1)} %broadcast_in_dim.8), calls=%async_computation.2 | async-start | bytes 1048576 | tf_op jit(solution)/shard_map/all_to_all | solution.py:281
  48.1 48.4 %collective-permute-start.3 = (bf16[192,1024]{1,0:T(8,128)(2,1)}, bf16[192,1024]{1,0:T(8,128)(2,1)}, u32[]{:S(2)}, u32[]{:S(2)}) collective-permute-start(bf16[192,1024]{1,0:T(8,128)(2,1)} %get-tuple-element.12), channel_id=1, source_target_pairs={{64,32},{32,64},{128,96},{96,128},{192,160},{160,192},{256,224},{2... | collective-permute-start | bytes 1179656 | tf_op jit(solution)/shard_map/ppermute | solution.py:277
  52.0 44.5 %collective-permute-start.4 = (bf16[192,1024]{1,0:T(8,128)(2,1)}, bf16[192,1024]{1,0:T(8,128)(2,1)}, u32[]{:S(2)}, u32[]{:S(2)}) collective-permute-start(bf16[192,1024]{1,0:T(8,128)(2,1)} %get-tuple-element.13), channel_id=1, source_target_pairs={{32,0},{0,32},{96,64},{64,96},{160,128},{128,160},{224,192},{192,2... | collective-permute-start | bytes 1179656 | tf_op jit(solution)/shard_map/ppermute | solution.py:277
  54.0 19.9 %collective-permute-start.7 = (bf16[64,1024]{1,0:T(8,128)(2,1)}, bf16[64,1024]{1,0:T(8,128)(2,1)}, u32[]{:S(2)}, u32[]{:S(2)}) collective-permute-start(bf16[64,1024]{1,0:T(8,128)(2,1)} %get-tuple-element.14.refs_8_.refs_9_), channel_id=1, source_target_pairs={{128,64},{160,96},{64,128},{96,160},{256,192},{288,224},{192,256},... | collective-permute-start | bytes 393224 | tf_op jit(solution)/shard_map/ppermute | solution.py:277
  58.2 52.1 %collective-permute-start = (bf16[256,1024]{1,0:T(8,128)(2,1)}, bf16[256,1024]{1,0:T(8,128)(2,1)}, u32[]{:S(2)}, u32[]{:S(2)}) collective-permute-start(bf16[256,1024]{1,0:T(8,128)(2,1)} %bitcast.3.refs_2_.refs_3_), channel_id=1, source_target_pairs={{1,0},{33,32},{65,64},{97,96},{129,128},{161,160},{193,192},{225,2... | collective-permute-start | bytes 1572872 | tf_op jit(solution)/shard_map/ppermute | solution.py:277
  65.6 11.2 %collective-permute-start.6 = (bf16[64,1024]{1,0:T(8,128)(2,1)}, bf16[64,1024]{1,0:T(8,128)(2,1)}, u32[]{:S(2)}, u32[]{:S(2)}) collective-permute-start(bf16[64,1024]{1,0:T(8,128)(2,1)} %get-tuple-element.14.refs_8_.refs_9_), channel_id=1, source_target_pairs={{96,0},{160,64},{0,96},{224,128},{64,160},{288,192},{128,224},{352... | collective-permute-start | bytes 393224 | tf_op jit(solution)/shard_map/ppermute | solution.py:277
  73.8 11.5 %collective-permute-start.5 = (bf16[64,1024]{1,0:T(8,128)(2,1)}, bf16[64,1024]{1,0:T(8,128)(2,1)}, u32[]{:S(2)}, u32[]{:S(2)}) collective-permute-start(bf16[64,1024]{1,0:T(8,128)(2,1)} %get-tuple-element.14.refs_8_.refs_9_), channel_id=1, source_target_pairs={{64,0},{96,32},{0,64},{32,96},{192,128},{224,160},{128,192},{160,2... | collective-permute-start | bytes 393224 | tf_op jit(solution)/shard_map/ppermute | solution.py:277
  76.8 33.5 %collective-permute-start.2 = (bf16[128,1024]{1,0:T(8,128)(2,1)}, bf16[128,1024]{1,0:T(8,128)(2,1)}, u32[]{:S(2)}, u32[]{:S(2)}) collective-permute-start(bf16[128,1024]{1,0:T(8,128)(2,1)} %bitcast.5), channel_id=1, source_target_pairs={{2,1},{34,33},{66,65},{98,97},{130,129},{162,161},{194,193},{226,2... | collective-permute-start | bytes 786440 | tf_op jit(solution)/shard_map/ppermute | solution.py:277
  85.3 25.0 %collective-permute-start.1 = (bf16[128,1024]{1,0:T(8,128)(2,1)}, bf16[128,1024]{1,0:T(8,128)(2,1)}, u32[]{:S(2)}, u32[]{:S(2)}) collective-permute-start(bf16[128,1024]{1,0:T(8,128)(2,1)} %bitcast.6), channel_id=1, source_target_pairs={{1,0},{33,32},{65,64},{97,96},{129,128},{161,160},{193,192},{225,2... | collective-permute-start | bytes 786440 | tf_op jit(solution)/shard_map/ppermute | solution.py:277

commit v2 on v1

--- a/solution.py
+++ b/solution.py
@@ -306,10 +306,9 @@
     far = moved(first, lambda i: i - 2 if i % 4 < 2 else i + 2)
 
     top = exchanged(pool_again(group, 4), "z_hi")
-    top = exchanged(jnp.broadcast_to(top[None], (4, *top.shape)), "x")
+    top = exchanged(jnp.broadcast_to(top[None], (8, *top.shape)), ("x", "core"))
     group_pair = moved(group, lambda i: i ^ SEQ)
     group_other = moved(group, lambda i: i + SEQ if (i // SEQ) % 2 else i - SEQ)
-    top_pair = moved(top, lambda i: i ^ SEQ)
 
     def both(array):
         return (array, 0, array, KVHEADS)
@@ -319,9 +318,11 @@
 
     rows = keys.shape[0]
     firsts = first.shape[0]
-    near = [(keys, 0, values, 0)] + [both(a) for a in (other, partner, first, two, third, far)]
+    near = [(keys, 0, values, 0)]
+    near += [both(a) for a in (other, partner, first, two, third, far, group, group_pair)]
     pieces = [(1, 0, BLOCK), (0, 0, rows), (2, 0, BLOCK), (3, 0, firsts), (2, BLOCK, firsts)]
     pieces += [(1, BLOCK, firsts), (4, 0, firsts), (5, 0, firsts), (6, 0, firsts)]
+    pieces += [(k, 0, BLOCK) for k in (7, 8)]
     part, lse = attend(
         flags,
         queries,
@@ -329,21 +330,20 @@
         pieces,
         [0, 2],
         {0: (0, 1), 2: (1, 1), 5: (4, 3), 7: (6, 3), 8: (2, 3)},
-        lambda b: [(b * BLOCK, 3 * BLOCK), (rows + 2 * BLOCK, 3 * BLOCK)],
-        6 * BLOCK,
+        lambda b: [(b * BLOCK, 3 * BLOCK), (rows + 2 * BLOCK, 5 * BLOCK)],
+        8 * BLOCK,
         later=True,
     )
-    coarse = [both(a) for a in (top, top_pair, group, group_pair, group_other)]
-    tops = 2 * top.shape[0]
+    coarse = [both(top), both(group_other)]
     (out,) = attend(
         flags,
         queries,
         coarse,
         whole(coarse),
         [],
-        {4: (3, 2)},
-        lambda b: [(0, tops + 3 * BLOCK)],
-        tops + 3 * BLOCK,
+        {1: (3, 0)},
+        lambda b: [(0, top.shape[0] + BLOCK)],
+        top.shape[0] + BLOCK,
         before=(part, lse),
     )
     return out

time: 127 us -> 130 us (1.024)
  the two profiles are of different devices: /device:TPU:111 before, /device:TPU:1 now
where the time goes in v2:
time: 130 us; the launch traced here: 128 us
  blocking collectives  44.5 us (34%)
  Pallas kernels  34.5 us (27%)
  starting transfers between devices  27.3 us (21%)
  waiting for transfers between devices  19.2 us (15%)
  local copies, waits for them, and re-layouts  2.67 us (2%)
    all_to_all x2, blocking collectives, exchanged(): result = lax.all_to_all(copies, axis, 0, 0, tiled=True)  44.5 us
    pallas_call x2, Pallas kernels, attend(): pl.pallas_call(functools.partial(attend_kernel, len(sources), pieces, swa...  29.8 us
    ppermute x7, starting transfers between devices, moved(): return lax.ppermute(rows, FINE, route)  20 us
    ppermute x7, waiting for transfers between devices, moved(): return lax.ppermute(rows, FINE, route)  19.2 us
    all_to_all x1, starting transfers between devices, exchanged(): result = lax.all_to_all(copies, axis, 0, 0, tiled=True)  7.24 us
    pallas_call x1, Pallas kernels, pool_local(): pl.pallas_call(pool_kernel, in_specs=[pl.BlockSpec(memory_space=pltpu.SME...  2.92 us
  transfers between devices with their start and end apart: 8, of which 2 were waited for; matrix products, arithmetic and copies ran while one was open for 0% of the time, Pallas kernels for 14%

profile of v2, /device:TPU:1, one launch (start us, length us, event | category | flops | bytes accessed | tf_op | source)
XLA Modules:
  0.0 128.3 jit_solution(8065153853206141718)
XLA Ops:
  0.0 2.9 %pool_local.1 = (bf16[64,1024]{1,0:T(8,128)(2,1)}, bf16[16,8,1024]{2,1,0:T(8,128)(2,1)}, bf16[192,1024]{1,0:T(8,128)(2,1)}, bf16[192,1024]{1,0:T(8,128)(2,1)}) custom-call(s32[1]{0:T(128)} %bitcast.flags.refs_0_, bf16[512,512]{1,0:T(8,128)(2,1)} %refs_2_.1, bf16[512,512]{1,0:T(8,128)(2,1)} %refs_3_.1), custom_call_target="tpu_custom_call" | custom-call | tf_op jit(solution)/shard_map/pool_local/pallas_call | solution.py:71
  2.9 17.9 %all_to_all.15 = bf16[16,8,1024]{2,1,0:T(8,128)(2,1)} all-to-all(bf16[16,8,1024]{2,1,0:T(8,128)(2,1)} %get-tuple-element.11), channel_id=1, replica_groups=mesh['y'=4,'z_lo'=4,'z_hi'=4,'x'=4,'core'=2] {'y','z_lo'}, dimensions={0} | all-to-all | bytes 524288 | tf_op jit(solution)/shard_map/all_to_all | solution.py:281
  20.8 1.8 %pool_again.1 = bf16[4,16,1024]{2,1,0:T(8,128)(2,1)} custom-call(bf16[128,1024]{1,0:T(8,128)(2,1)} %bitcast.1.rows_ref.refs_16_.refs_17_), custom_call_target="tpu_custom_call" | custom-call | tf_op jit(solution)/shard_map/pool_again/pallas_call | solution.py:87
  22.6 26.6 %all_to_all.16 = bf16[4,16,1024]{2,1,0:T(8,128)(2,1)S(1)} all-to-all(bf16[4,16,1024]{2,1,0:T(8,128)(2,1)} %pool_again.1), channel_id=1, replica_groups=mesh['y'=4,'z_lo'=4,'z_hi'=4,'x'=4,'core'=2] {'z_hi'}, dimensions={0} | all-to-all | bytes 262144 | tf_op jit(solution)/shard_map/all_to_all | solution.py:281
  49.2 1.1 broadcast_in_dim.8
  50.3 7.2 %all-to-all-start.2 = ((bf16[8,64,1024]{2,1,0:T(8,128)(2,1)}), bf16[8,64,1024]{2,1,0:T(8,128)(2,1)}, u32[]{:S(2)}, u32[]{:S(2)}) async-start(bf16[8,64,1024]{2,1,0:T(8,128)(2,1)} %broadcast_in_dim.8), calls=%async_computation.2 | async-start | bytes 2097152 | tf_op jit(solution)/shard_map/all_to_all | solution.py:281
  57.5 3.3 %collective-permute-start.1 = (bf16[192,1024]{1,0:T(8,128)(2,1)S(1)}, bf16[192,1024]{1,0:T(8,128)(2,1)S(1)}, u32[]{:S(2)}, u32[]{:S(2)}) collective-permute-start(bf16[192,1024]{1,0:T(8,128)(2,1)S(1)} %copy-done.1), channel_id=1, source_target_pairs={{64,32},{32,64},{128,96},{96,128},{192,160},{160,192},{256,224},{2... | collective-permute-start | bytes 1179656 | tf_op jit(solution)/shard_map/ppermute | solution.py:277
  60.9 1.9 %collective-permute-start.2 = (bf16[192,1024]{1,0:T(8,128)(2,1)S(1)}, bf16[192,1024]{1,0:T(8,128)(2,1)S(1)}, u32[]{:S(2)}, u32[]{:S(2)}) collective-permute-start(bf16[192,1024]{1,0:T(8,128)(2,1)S(1)} %copy-done), channel_id=1, source_target_pairs={{32,0},{0,32},{96,64},{64,96},{160,128},{128,160},{224,192},{192,2... | collective-permute-start | bytes 1179656 | tf_op jit(solution)/shard_map/ppermute | solution.py:277
  62.8 6.7 %collective-permute-start.5 = (bf16[64,1024]{1,0:T(8,128)(2,1)S(1)}, bf16[64,1024]{1,0:T(8,128)(2,1)S(1)}, u32[]{:S(2)}, u32[]{:S(2)}) collective-permute-start(bf16[64,1024]{1,0:T(8,128)(2,1)S(1)} %copy-done.4), channel_id=1, source_target_pairs={{128,64},{160,96},{64,128},{96,160},{256,192},{288,224},{192,256},... | collective-permute-start | bytes 393224 | tf_op jit(solution)/shard_map/ppermute | solution.py:277
  69.5 1.9 %collective-permute-start.6 = (bf16[128,1024]{1,0:T(8,128)(2,1)}, bf16[128,1024]{1,0:T(8,128)(2,1)}, u32[]{:S(2)}, u32[]{:S(2)}) collective-permute-start(bf16[128,1024]{1,0:T(8,128)(2,1)} %bitcast.1.rows_ref.refs_16_.refs_17_), channel_id=1, source_target_pairs={{1,0},{33,32},{65,64},{97,96},{129,128},{161,160},{193,192},{225,2... | collective-permute-start | bytes 786440 | tf_op jit(solution)/shard_map/ppermute | solution.py:277
  71.4 2.3 %collective-permute-start.4 = (bf16[64,1024]{1,0:T(8,128)(2,1)S(1)}, bf16[64,1024]{1,0:T(8,128)(2,1)S(1)}, u32[]{:S(2)}, u32[]{:S(2)}) collective-permute-start(bf16[64,1024]{1,0:T(8,128)(2,1)S(1)} %copy-done.4), channel_id=1, source_target_pairs={{96,0},{160,64},{0,96},{224,128},{64,160},{288,192},{128,224},{352... | collective-permute-start | bytes 393224 | tf_op jit(solution)/shard_map/ppermute | solution.py:277
  73.8 15.9 %collective-permute-done.5.refs_14_.refs_15_ = bf16[64,1024]{1,0:T(8,128)(2,1)S(1)} collective-permute-done((bf16[64,1024]{1,0:T(8,128)(2,1)S(1)}, bf16[64,1024]{1,0:T(8,128)(2,1)S(1)}, u32[]{:S(2)}, u32[]{:S(2)}) %collective-permute-start.5) | collective-permute-done | bytes 131104 | tf_op jit(solution)/shard_map/ppermute | solution.py:277
  89.6 1.9 %collective-permute-start.3 = (bf16[64,1024]{1,0:T(8,128)(2,1)S(1)}, bf16[64,1024]{1,0:T(8,128)(2,1)S(1)}, u32[]{:S(2)}, u32[]{:S(2)}) collective-permute-start(bf16[64,1024]{1,0:T(8,128)(2,1)S(1)} %copy-done.4), channel_id=1, source_target_pairs={{64,0},{96,32},{0,64},{32,96},{192,128},{224,160},{128,192},{160,2... | collective-permute-start | bytes 393224 | tf_op jit(solution)/shard_map/ppermute | solution.py:277
  91.5 0.0 collective-permute-done.4.refs_12_.refs_13_
  91.6 1.9 %collective-permute-start = (bf16[128,1024]{1,0:T(8,128)(2,1)}, bf16[128,1024]{1,0:T(8,128)(2,1)}, u32[]{:S(2)}, u32[]{:S(2)}) collective-permute-start(bf16[128,1024]{1,0:T(8,128)(2,1)} %bitcast.1.rows_ref.refs_16_.refs_17_), channel_id=1, source_target_pairs={{2,1},{34,33},{66,65},{98,97},{130,129},{162,161},{194,193},{226,2... | collective-permute-start | bytes 786440 | tf_op jit(solution)/shard_map/ppermute | solution.py:277
  93.5 3.3 %collective-permute-done.3.refs_10_.refs_11_ = bf16[64,1024]{1,0:T(8,128)(2,1)S(1)} collective-permute-done((bf16[64,1024]{1,0:T(8,128)(2,1)S(1)}, bf16[64,1024]{1,0:T(8,128)(2,1)S(1)}, u32[]{:S(2)}, u32[]{:S(2)}) %collective-permute-start.3) | collective-permute-done | bytes 131104 | tf_op jit(solution)/shard_map/ppermute | solution.py:277
  96.8 0.0 collective-permute-done.1.refs_4_.refs_5_
  96.9 0.6 copy-done.7
  97.5 0.2 copy-done.2
  97.6 0.8 copy-done.3
  98.4 0.0 collective-permute-done.6.refs_18_.refs_19_
  98.4 17.5 %shard_map.37 = (bf16[512,2048]{1,0:T(8,128)(2,1)}, f32[8192,128]{1,0:T(8,128)}) custom-call(s32[1]{0:T(128)} %bitcast.flags.refs_0_, bf16[512,2048]{1,0:T(8,128)(2,1)} %refs_1_.3, bf16[512,512]{1,0:T(8,128)(2,1)} %refs_2_.1, bf16[512,512]{1,0:T(8,128)(2,1)} %refs_3_.1, bf16[192,1024]{1,0:T(8,128)(2,1)} %copy-done.2, bf16[192,1024]{1,0:T(8,128)(2,1)} %copy-done.2, ...), custom_call_target="tpu_custom_call" | custom-call | flops 4294967296 | bytes 6291456 | tf_op jit(solution)/shard_map/pallas_call | solution.py:243
  115.9 0.0 collective-permute-done.refs_4_.refs_5_
  115.9 12.4 %shard_map.38 = bf16[512,2048]{1,0:T(8,128)(2,1)} custom-call(s32[1]{0:T(128)} %bitcast.flags.refs_0_, bf16[512,2048]{1,0:T(8,128)(2,1)} %refs_1_.3, bf16[512,1024]{1,0:T(8,128)(2,1)} %bitcast.3.refs_2_.refs_3_, bf16[512,1024]{1,0:T(8,128)(2,1)} %bitcast.3.refs_2_.refs_3_, bf16[128,1024]{1,0:T(8,128)(2,1)} %collective-permute-done.refs_4_.refs_5_, ...), custom_call_target="tpu_custom_call" | custom-call | flops 2684354560 | bytes 6291456 | tf_op jit(solution)/shard_map/pallas_call | solution.py:243
  (15 shorter events, 0.0 us)
Async XLA Ops:
  22.5 35.0 %copy-start.1 = (bf16[192,1024]{1,0:T(8,128)(2,1)S(1)}, bf16[192,1024]{1,0:T(8,128)(2,1)}, u32[]{:S(2)}) copy-start(bf16[192,1024]{1,0:T(8,128)(2,1)} %get-tuple-element.12) | copy-start | bytes 1179652
  22.5 38.3 %copy-start = (bf16[192,1024]{1,0:T(8,128)(2,1)S(1)}, bf16[192,1024]{1,0:T(8,128)(2,1)}, u32[]{:S(2)}) copy-start(bf16[192,1024]{1,0:T(8,128)(2,1)} %get-tuple-element.13) | copy-start | bytes 1179652
  22.6 40.3 %copy-start.4 = (bf16[64,1024]{1,0:T(8,128)(2,1)S(1)}, bf16[64,1024]{1,0:T(8,128)(2,1)}, u32[]{:S(2)}) copy-start(bf16[64,1024]{1,0:T(8,128)(2,1)} %get-tuple-element.14.refs_8_.refs_9_) | copy-start | bytes 393220
  50.3 65.6 %all-to-all-start.2 = ((bf16[8,64,1024]{2,1,0:T(8,128)(2,1)}), bf16[8,64,1024]{2,1,0:T(8,128)(2,1)}, u32[]{:S(2)}, u32[]{:S(2)}) async-start(bf16[8,64,1024]{2,1,0:T(8,128)(2,1)} %broadcast_in_dim.8), calls=%async_computation.2 | async-start | bytes 2097152 | tf_op jit(solution)/shard_map/all_to_all | solution.py:281
  57.5 39.3 %collective-permute-start.1 = (bf16[192,1024]{1,0:T(8,128)(2,1)S(1)}, bf16[192,1024]{1,0:T(8,128)(2,1)S(1)}, u32[]{:S(2)}, u32[]{:S(2)}) collective-permute-start(bf16[192,1024]{1,0:T(8,128)(2,1)S(1)} %copy-done.1), channel_id=1, source_target_pairs={{64,32},{32,64},{128,96},{96,128},{192,160},{160,192},{256,224},{2... | collective-permute-start | bytes 1179656 | tf_op jit(solution)/shard_map/ppermute | solution.py:277
  60.9 36.0 %collective-permute-start.2 = (bf16[192,1024]{1,0:T(8,128)(2,1)S(1)}, bf16[192,1024]{1,0:T(8,128)(2,1)S(1)}, u32[]{:S(2)}, u32[]{:S(2)}) collective-permute-start(bf16[192,1024]{1,0:T(8,128)(2,1)S(1)} %copy-done), channel_id=1, source_target_pairs={{32,0},{0,32},{96,64},{64,96},{160,128},{128,160},{224,192},{192,2... | collective-permute-start | bytes 1179656 | tf_op jit(solution)/shard_map/ppermute | solution.py:277
  62.8 26.8 %collective-permute-start.5 = (bf16[64,1024]{1,0:T(8,128)(2,1)S(1)}, bf16[64,1024]{1,0:T(8,128)(2,1)S(1)}, u32[]{:S(2)}, u32[]{:S(2)}) collective-permute-start(bf16[64,1024]{1,0:T(8,128)(2,1)S(1)} %copy-done.4), channel_id=1, source_target_pairs={{128,64},{160,96},{64,128},{96,160},{256,192},{288,224},{192,256},... | collective-permute-start | bytes 393224 | tf_op jit(solution)/shard_map/ppermute | solution.py:277
  69.5 28.9 %collective-permute-start.6 = (bf16[128,1024]{1,0:T(8,128)(2,1)}, bf16[128,1024]{1,0:T(8,128)(2,1)}, u32[]{:S(2)}, u32[]{:S(2)}) collective-permute-start(bf16[128,1024]{1,0:T(8,128)(2,1)} %bitcast.1.rows_ref.refs_16_.refs_17_), channel_id=1, source_target_pairs={{1,0},{33,32},{65,64},{97,96},{129,128},{161,160},{193,192},{225,2... | collective-permute-start | bytes 786440 | tf_op jit(solution)/shard_map/ppermute | solution.py:277
  71.4 20.1 %collective-permute-start.4 = (bf16[64,1024]{1,0:T(8,128)(2,1)S(1)}, bf16[64,1024]{1,0:T(8,128)(2,1)S(1)}, u32[]{:S(2)}, u32[]{:S(2)}) collective-permute-start(bf16[64,1024]{1,0:T(8,128)(2,1)S(1)} %copy-done.4), channel_id=1, source_target_pairs={{96,0},{160,64},{0,96},{224,128},{64,160},{288,192},{128,224},{352... | collective-permute-start | bytes 393224 | tf_op jit(solution)/shard_map/ppermute | solution.py:277
  89.6 7.2 %copy-start.5 = (bf16[64,1024]{1,0:T(8,128)(2,1)}, bf16[64,1024]{1,0:T(8,128)(2,1)S(1)}, u32[]{:S(2)}) copy-start(bf16[64,1024]{1,0:T(8,128)(2,1)S(1)} %collective-permute-done.5.refs_14_.refs_15_) | copy-start | bytes 393220
  89.6 7.2 %collective-permute-start.3 = (bf16[64,1024]{1,0:T(8,128)(2,1)S(1)}, bf16[64,1024]{1,0:T(8,128)(2,1)S(1)}, u32[]{:S(2)}, u32[]{:S(2)}) collective-permute-start(bf16[64,1024]{1,0:T(8,128)(2,1)S(1)} %copy-done.4), channel_id=1, source_target_pairs={{64,0},{96,32},{0,64},{32,96},{192,128},{224,160},{128,192},{160,2... | collective-permute-start | bytes 393224 | tf_op jit(solution)/shard_map/ppermute | solution.py:277
  91.6 5.3 %copy-start.6 = (bf16[64,1024]{1,0:T(8,128)(2,1)}, bf16[64,1024]{1,0:T(8,128)(2,1)S(1)}, u32[]{:S(2)}) copy-start(bf16[64,1024]{1,0:T(8,128)(2,1)S(1)} %collective-permute-done.4.refs_12_.refs_13_) | copy-start | bytes 393220
  91.6 24.3 %collective-permute-start = (bf16[128,1024]{1,0:T(8,128)(2,1)}, bf16[128,1024]{1,0:T(8,128)(2,1)}, u32[]{:S(2)}, u32[]{:S(2)}) collective-permute-start(bf16[128,1024]{1,0:T(8,128)(2,1)} %bitcast.1.rows_ref.refs_16_.refs_17_), channel_id=1, source_target_pairs={{2,1},{34,33},{66,65},{98,97},{130,129},{162,161},{194,193},{226,2... | collective-permute-start | bytes 786440 | tf_op jit(solution)/shard_map/ppermute | solution.py:277
  96.8 0.6 copy-start.7
  96.8 0.8 copy-start.2
  97.6 0.8 copy-start.3
